TPU v7x, 32 devices: a whole 2x2x4 slice. The times are simulated.
32 devices in a mesh: group: 2 (over x), seq: 16 (over z, y, core).
Axes of the slice: x: 2, y: 2, z: 4, core: 2. Of those that a mesh axis runs over, the one named last changes fastest.
Arguments:
- tokens: bfloat16 [16384, 4096], P(('group', 'seq')), parts along dimension 0, may hold values from -6 to 6
- norm_gain: bfloat16 [4096], replicated, may hold values from 0.099609375 to 1.8984375
- w_key: bfloat16 [4096, 1024], P('seq'), may hold values from -0.09375 to 0.09375
- w_value: bfloat16 [4096, 1024], P('seq'), may hold values from -0.09375 to 0.09375
- lengths: int32 [4], P('group'), parts along dimension 0, may hold values from 2048 to 4096
- page_table: int32 [1024], P(('group', 'seq')), parts along dimension 0, may hold values from 0 to 639, as said below
Outputs:
- kv_cache: bfloat16 [2, 1280, 16, 1024], P(None, ('group', 'seq')), parts along dimension 1
There are 2 independent parts, one for each index of `group`. A program takes and returns all parts, laid end to end along the dimension named above; an argument that names none is the same for every part. Nothing has to cross between parts.
Inputs may be any that keep to these rules, and one draw needn't show every extreme that they name: The entries are distinct. Page g of the 32 pages of device s goes to slot page_table[g] of decode device page_table[g] // 40, which is s + k modulo 16 for an offset k in -2 .. 2, at a slot of the block of 8 slots from (k + 2) * 8 on; so at most 8 pages go from one device to one decode device, and exactly 8 from every device to some decode device.
All inputs are finite; a program needn't handle non-finite values.
Results may differ from a plain program's by a relative error of at most 0.0049.
Values may be sent and summed in bfloat16 or wider, within the bound.
A program may use at most 64 MiB of HBM per device.

v0:
```python
import jax
import jax.numpy as jnp
from jax import lax
from jax.sharding import PartitionSpec as P

HEAD = 128
PAGE = 16
REACH = 2
CAP = 8
SLOTS = 40


ROPE_THETA = 500000.0
EPS = 1e-05


def shifted(block, axis, distance):
    devices = range(lax.axis_size(axis))
    route = [((i - distance) % len(devices), i) for i in devices]
    return lax.ppermute(block, axis, route)


def rotate_keys(key_rows, position):
    half = HEAD // 2
    freq = ROPE_THETA ** (-(jnp.arange(half, dtype=jnp.float32) * 2.0 / HEAD))
    angle = position.astype(jnp.float32)[:, None] * freq[None, :]
    cosine = jnp.cos(angle)[:, None, :]
    sine = jnp.sin(angle)[:, None, :]
    shaped = key_rows.reshape(key_rows.shape[0], -1, HEAD)
    first = shaped[:, :, :half]
    second = shaped[:, :, half:]
    turned = jnp.concatenate(
        [first * cosine - second * sine, second * cosine + first * sine], axis=2
    )
    return turned.reshape(key_rows.shape)


def hand_over(placed):
    regions = [
        placed[:, (offset + REACH) * CAP : (offset + REACH + 1) * CAP]
        for offset in range(-REACH, REACH + 1)
    ]
    arrived = []
    for offset in range(-REACH, REACH + 1):
        if offset == 0:
            arrived.append(regions[REACH])
        else:
            arrived.append(shifted(regions[offset + REACH], "seq", offset))
    return jnp.concatenate(arrived, axis=1)


def on_device(tokens, norm_gain, w_key, w_value, lengths, page_table):
    axis_size = lax.axis_size("seq")
    device_index = lax.axis_index("seq")
    tok_rows = tokens.shape[0]
    length_each = tok_rows * axis_size // 2
    token_index = device_index * tok_rows + jnp.arange(tok_rows, dtype=jnp.int32)
    prompt_id = token_index // length_each
    position = token_index % length_each
    limit = jnp.where(prompt_id == 0, lengths[0], lengths[1])
    inside = (position < limit)[:, None]
    wide = tokens.astype(jnp.float32)
    scale = lax.rsqrt(jnp.mean(wide * wide, axis=1, keepdims=True) + EPS)
    normed = (wide * scale * norm_gain.astype(jnp.float32)[None, :]).astype(jnp.bfloat16)
    page_count = tok_rows // PAGE
    local_slot = page_table % SLOTS
    slot_onehot = (jnp.arange(SLOTS, dtype=jnp.int32)[:, None] == local_slot[None, :]).astype(
        jnp.bfloat16
    )
    key_whole, value_whole = (
        lax.all_gather(w_key, "seq", axis=0, tiled=True),
        lax.all_gather(w_value, "seq", axis=0, tiled=True),
    )
    key_rows = jnp.dot(normed, key_whole, preferred_element_type=jnp.float32)
    value_rows = jnp.dot(normed, value_whole, preferred_element_type=jnp.float32)
    columns = key_rows.shape[1]
    keys = jnp.where(inside, rotate_keys(key_rows, position), 0.0).astype(jnp.bfloat16)
    values = jnp.where(inside, value_rows, 0.0).astype(jnp.bfloat16)
    stacked = jnp.stack([keys, values]).reshape(2, page_count, PAGE * columns)
    placed = jnp.einsum(
        "sp,cpx->csx", slot_onehot, stacked, preferred_element_type=jnp.float32
    ).astype(jnp.bfloat16)
    return hand_over(placed).reshape(2, SLOTS, PAGE, columns)


def solution(mesh):
    placed = (
        P(("group", "seq"), None),
        P(),
        P("seq", None),
        P("seq", None),
        P("group"),
        P(("group", "seq")),
    )
    return jax.shard_map(
        on_device,
        mesh=mesh,
        in_specs=placed,
        out_specs=P(None, ("group", "seq"), None, None),
        check_vma=False,
    )
```

profile of v0, /device:TPU:1, one launch (start us, length us, event | category | flops | bytes accessed | tf_op | source)
XLA Modules:
  0.0 226.1 jit_solution(9761651501700079864)
XLA Ops:
  6.5 0.7 all-gather.3.cloned.1.call-update
  7.3 0.7 all-gather.5.cloned.1.call-update
  8.0 0.7 convert_element_type.38
  8.7 1.4 fusion.20
  10.1 1.3 select_compare_fusion
  11.6 0.6 broadcast_in_dim.42
  12.2 3.1 %fusion.1 = f32[512]{0:T(512)S(1)} fusion(bf16[512,4096]{1,0:T(8,128)(2,1)} %param.6), kind=kLoop, calls=%fused_computation.4 | loop fusion | flops 6290944 | bytes 4196352 | tf_op jit(solution)/shard_map/reduce_sum | solution.py:63
  15.3 1.0 multiply_cosine_fusion
  16.3 70.0 %all-gather.3.cloned.1.call-done = bf16[4096,1024]{1,0:T(8,128)(2,1)} async-done(((bf16[256,1024]{1,0:T(8,128)(2,1)}), bf16[4096,1024]{1,0:T(8,128)(2,1)}) %all-gather.3.cloned.1.call-update) | async-done | bytes 8388624 | tf_op jit(solution)/shard_map/all_gather | solution.py:71
  86.3 8.2 %convolution_bitcast_fusion = f32[64,8,8,128]{3,1,2,0:T(8,128)S(1)} fusion(bf16[4096,1024]{1,0:T(8,128)(2,1)} %all-gather.3.cloned.1.call-done, bf16[512,4096]{1,0:T(8,128)(2,1)} %param.6, f32[4096]{0:T(1024)S(1)} %convert_element_type.38, f32[512]{0:T(512)S(1)} %add_rsqrt_fusion), kind=kOutput, calls=%fused_computation.15 | convolution fusion | flops 4303355904 | bytes 14698496 | tf_op jit(solution)/shard_map/dot_general | solution.py:74
  95.0 0.8 multiply_subtract_fusion
  95.8 0.6 pad_maximum_fusion
  96.9 64.5 %all-gather.5.cloned.1.call-done = bf16[4096,1024]{1,0:T(8,128)(2,1)} async-done(((bf16[256,1024]{1,0:T(8,128)(2,1)}), bf16[4096,1024]{1,0:T(8,128)(2,1)}) %all-gather.5.cloned.1.call-update) | async-done | bytes 8388624 | tf_op jit(solution)/shard_map/all_gather | solution.py:72
  161.4 10.2 %select_convert_fusion = bf16[512,1024]{1,0:T(8,128)(2,1)} fusion(bf16[4096,1024]{1,0:T(8,128)(2,1)} %all-gather.5.cloned.1.call-done, bf16[512,4096]{1,0:T(8,128)(2,1)} %param.6, f32[4096]{0:T(1024)S(1)} %convert_element_type.38, f32[512]{0:T(512)S(1)} %add_rsqrt_fusion, pred[512]{0:T(512)(128)(4,1)S(1)} %select_compare_fusion), kind=kOutput, calls=%fused_computation.11 | convolution fusion | flops 4304404480 | bytes 13650432 | tf_op jit(solution)/shard_map/dot_general | solution.py:75
  171.5 1.6 stack.7
  173.4 1.0 fusion
  174.5 1.7 collective-permute-start
  176.1 0.5 collective-permute-start.1
  176.7 11.1 %collective-permute-done = bf16[2,8,16384]{2,1,0:T(8,128)(2,1)S(1)} collective-permute-done((bf16[2,8,16384]{2,1,0:T(8,128)(2,1)S(1)}, bf16[2,8,16384]{2,1,0:T(8,128)(2,1)S(1)}, u32[]{:S(2)}, u32[]{:S(2)}) %collective-permute-start) | collective-permute-done | bytes 524320 | tf_op jit(solution)/shard_map/ppermute | solution.py:20
  187.8 6.0 %collective-permute-done.1 = bf16[2,8,16384]{2,1,0:T(8,128)(2,1)S(1)} collective-permute-done((bf16[2,8,16384]{2,1,0:T(8,128)(2,1)S(1)}, bf16[2,8,16384]{2,1,0:T(8,128)(2,1)S(1)}, u32[]{:S(2)}, u32[]{:S(2)}) %collective-permute-start.1) | collective-permute-done | bytes 524320 | tf_op jit(solution)/shard_map/ppermute | solution.py:20
  194.0 1.2 collective-permute-start.3
  195.2 8.4 %collective-permute-done.2 = bf16[2,8,16384]{2,1,0:T(8,128)(2,1)S(1)} collective-permute-done((bf16[2,8,16384]{2,1,0:T(8,128)(2,1)S(1)}, bf16[2,8,16384]{2,1,0:T(8,128)(2,1)S(1)}, u32[]{:S(2)}, u32[]{:S(2)}) %collective-permute-start.2) | collective-permute-done | bytes 524320 | tf_op jit(solution)/shard_map/ppermute | solution.py:20
  203.6 12.5 %collective-permute-done.3 = bf16[2,8,16384]{2,1,0:T(8,128)(2,1)S(1)} collective-permute-done((bf16[2,8,16384]{2,1,0:T(8,128)(2,1)S(1)}, bf16[2,8,16384]{2,1,0:T(8,128)(2,1)S(1)}, u32[]{:S(2)}, u32[]{:S(2)}) %collective-permute-start.3) | collective-permute-done | bytes 524320 | tf_op jit(solution)/shard_map/ppermute | solution.py:20
  216.2 3.1 %copy.8 = bf16[10,8,16,1024]{3,2,1,0:T(8,128)(2,1)} copy(bf16[10,8,16,1024]{3,1,2,0:T(8,128)(2,1)S(1)} %bitcast.19) | data formatting | bytes 5242880
  (19 shorter events, 1.9 us)
Async XLA Ops:
  6.5 5.7 %copy-start = (s32[32]{0:T(128)S(1)}, s32[32]{0:T(128)}, u32[]{:S(2)}) copy-start(s32[32]{0:T(128)} %param.11) | copy-start | bytes 388
  6.5 79.8 %all-gather.3.cloned.1.call-start = ((), (), s32[]{:S(2)}) async-start(), calls=%async_computation | async-start | bytes 8912896 | tf_op jit(solution)/shard_map/all_gather | solution.py:71
  7.3 154.1 %all-gather.5.cloned.1.call-start = ((), (), s32[]{:S(2)}) async-start(), calls=%async_computation.1 | async-start | bytes 8912896 | tf_op jit(solution)/shard_map/all_gather | solution.py:72
  174.5 13.3 %collective-permute-start = (bf16[2,8,16384]{2,1,0:T(8,128)(2,1)S(1)}, bf16[2,8,16384]{2,1,0:T(8,128)(2,1)S(1)}, u32[]{:S(2)}, u32[]{:S(2)}) collective-permute-start(bf16[2,8,16384]{2,1,0:T(8,128)(2,1)S(1)} %get-tuple-element.9), channel_id=1, source_target_pairs={{2,0},{3,1},{4,2},{5,3},{6,4},{7,5},{8,6},{9,7},{10,8},{11,9},{12,... | collective-permute-start | bytes 1572872 | tf_op jit(solution)/shard_map/ppermute | solution.py:20
  176.1 17.6 %collective-permute-start.1 = (bf16[2,8,16384]{2,1,0:T(8,128)(2,1)S(1)}, bf16[2,8,16384]{2,1,0:T(8,128)(2,1)S(1)}, u32[]{:S(2)}, u32[]{:S(2)}) collective-permute-start(bf16[2,8,16384]{2,1,0:T(8,128)(2,1)S(1)} %get-tuple-element.8), channel_id=1, source_target_pairs={{1,0},{2,1},{3,2},{4,3},{5,4},{6,5},{7,6},{8,7},{9,8},{10,9},{11,1... | collective-permute-start | bytes 1572872 | tf_op jit(solution)/shard_map/ppermute | solution.py:20
  193.9 9.7 %collective-permute-start.2 = (bf16[2,8,16384]{2,1,0:T(8,128)(2,1)S(1)}, bf16[2,8,16384]{2,1,0:T(8,128)(2,1)S(1)}, u32[]{:S(2)}, u32[]{:S(2)}) collective-permute-start(bf16[2,8,16384]{2,1,0:T(8,128)(2,1)S(1)} %get-tuple-element.6), channel_id=1, source_target_pairs={{15,0},{0,1},{1,2},{2,3},{3,4},{4,5},{5,6},{6,7},{7,8},{8,9},{9,10... | collective-permute-start | bytes 1572872 | tf_op jit(solution)/shard_map/ppermute | solution.py:20
  194.0 22.2 %collective-permute-start.3 = (bf16[2,8,16384]{2,1,0:T(8,128)(2,1)S(1)}, bf16[2,8,16384]{2,1,0:T(8,128)(2,1)S(1)}, u32[]{:S(2)}, u32[]{:S(2)}) collective-permute-start(bf16[2,8,16384]{2,1,0:T(8,128)(2,1)S(1)} %get-tuple-element.5), channel_id=1, source_target_pairs={{14,0},{15,1},{0,2},{1,3},{2,4},{3,5},{4,6},{5,7},{6,8},{7,9},{8,1... | collective-permute-start | bytes 1572872 | tf_op jit(solution)/shard_map/ppermute | solution.py:20
Sparse Core Ops, SparseCore 0:
  9.5 76.7 all-gather.2
  88.5 72.8 all-gather.4
where the time goes:
time: 226 us
  waiting for transfers between devices  174 us (77%)
  matrix products  19.4 us (9%)
  between operations  13.5 us (6%)
  local copies, waits for them, and re-layouts  8.07 us (4%)
  other arithmetic  7.77 us (3%)
  starting transfers between devices  3.54 us (2%)
    all_gather x1, waiting for transfers between devices, on_device(): lax.all_gather(w_key, 'seq', axis=0, tiled=True)  70 us
    all_gather x1, waiting for transfers between devices, on_device(): lax.all_gather(w_value, 'seq', axis=0, tiled=True)  64.5 us
    ppermute x4, waiting for transfers between devices, shifted(): return lax.ppermute(block, axis, route)  38 us
    dot_general x1, matrix products, on_device(): jnp.dot(normed, value_whole, preferred_element_type=jnp.float32)  10.2 us
    dot_general x1, matrix products, on_device(): key_rows = jnp.dot(normed, key_whole, preferred_element_type=jnp.float32)  8.24 us
  transfers between devices with their start and end apart: 6, of which 6 were waited for; matrix products, arithmetic and copies ran while one was open for 8% of the time, Pallas kernels for 0%

commit v1 on v0

v1 whole, which is shorter than its diff:
```python
import functools

import jax
import jax.numpy as jnp
from jax import lax
from jax.experimental import pallas as pl
from jax.experimental.pallas import tpu as pltpu
from jax.sharding import PartitionSpec as P

HEAD = 128
PAGE = 16
REACH = 2
CAP = 8
SLOTS = 40
REGIONS = 2 * REACH + 1
BLOCK = CAP * PAGE
ROWS = SLOTS * PAGE

ROPE_THETA = 500000.0
EPS = 1e-05

CHUNKS = 4
TILE = 256
MESH = pl.DeviceIdType.MESH


def kernel(
    n, tokens, gain, w_key, w_value, dest, cosine, sine, out,
    wbuf, xbuf, pbuf, onehot,
    load_sem, tok_sem, zs, zr, ys, yr, xs, xr, ds, dr, cs, cr, hs, hr,
):
    chunks, depth = wbuf.shape[0], wbuf.shape[1]
    half, width = wbuf.shape[5], wbuf.shape[6]
    per_kind = chunks // 2
    tok_rows, features = xbuf.shape
    group = lax.axis_index("group")
    me = lax.axis_index("seq")
    core, y, z = lax.rem(me, 2), lax.rem(me // 2, 2), me // 4
    other_core, other_y, other_group = 1 - core, 1 - y, 1 - group

    def seq_of(z_at, y_at, core_at):
        return (z_at * 2 + y_at) * 2 + core_at

    def piece(j, z_at, y_at, part):
        return wbuf.at[j, z_at, y_at, core, part]

    def send(ref, send_sem, recv_sem, group_at, seq_at, dst=None):
        pltpu.make_async_remote_copy(
            src_ref=ref,
            dst_ref=ref if dst is None else dst,
            send_sem=send_sem,
            recv_sem=recv_sem,
            device_id={"group": group_at, "seq": seq_at},
            device_id_type=MESH,
        ).start()

    def wait(ref, sem):
        pltpu.make_async_copy(ref, ref, sem).wait()

    loads = []
    for j in range(chunks):
        w_ref = w_key if j < per_kind else w_value
        columns = pl.ds((j % per_kind) * width, width)
        for part in range(2):
            copy = pltpu.make_async_copy(
                w_ref.at[pl.ds(part * half, half), columns],
                wbuf.at[j, z, y, core, part],
                load_sem.at[j, part],
            )
            copy.start()
            loads.append(copy)
    token_copy = pltpu.make_async_copy(tokens, xbuf, tok_sem)
    token_copy.start()

    to_y = seq_of(z, other_y, core)
    to_core = seq_of(z, y, other_core)

    barrier = pltpu.get_barrier_semaphore()

    def greet(group_at, seq_at):
        pl.semaphore_signal(
            barrier, inc=1, device_id={"group": group_at, "seq": seq_at}, device_id_type=MESH
        )

    def greet_z(k, carry):
        greet(group, seq_of(lax.rem(z + k, depth), y, core))
        return carry

    lax.fori_loop(1, depth, greet_z, 0)
    greet(group, to_y)
    greet(group, to_core)
    greet(other_group, me)
    for region in range(REGIONS):
        if region != REACH:
            greet(group, lax.rem(me + region - REACH + n, n))
    pl.semaphore_wait(barrier, depth - 1 + 3 + REGIONS - 1)

    for copy in loads:
        copy.wait()

    def along_z(j):
        def body(k, carry):
            send(piece(j, z, y, group), zs.at[j], zr.at[j, z], group,
                 seq_of(lax.rem(z + k, depth), y, core))
            return carry

        lax.fori_loop(1, depth, body, 0)

    def to_partner(j, ref):
        send(ref, cs.at[j], cr.at[j], group, to_core)

    def spread(j):
        own = piece(j, z, y, group)
        send(own, ys.at[j], yr.at[j, z], group, to_y)
        to_partner(j, own)
        to_partner(j, piece(j, z, y, other_group))

        def body(k, carry):
            zz = lax.rem(z + k, depth)
            ref = piece(j, zz, y, group)
            wait(ref, zr.at[j, zz])
            send(ref, ys.at[j], yr.at[j, zz], group, to_y)
            send(ref, xs.at[j], xr.at[j, zz], other_group, me)
            to_partner(j, ref)
            return carry

        lax.fori_loop(1, depth, body, 0)

    def relay(j):
        def body(k, carry):
            zz = lax.rem(z + k, depth)
            ref = piece(j, zz, other_y, group)
            wait(ref, yr.at[j, zz])
            send(ref, ds.at[j], dr.at[j, zz], other_group, me)
            to_partner(j, ref)

            @pl.when(k > 0)
            def _():
                crossed = piece(j, zz, y, other_group)
                wait(crossed, xr.at[j, zz])
                to_partner(j, crossed)

            return carry

        lax.fori_loop(0, depth, body, 0)

    def finish(j):
        def body(k, carry):
            zz = lax.rem(z + k, depth)
            ref = piece(j, zz, other_y, other_group)
            wait(ref, dr.at[j, zz])
            to_partner(j, ref)
            return carry

        lax.fori_loop(0, depth, body, 0)
        wait(wbuf.at[j, :, :, other_core], cr.at[j])

    def normalise():
        token_copy.wait()

        def body(i, carry):
            rows = pl.ds(pl.multiple_of(i * 32, 32), 32)
            wide = xbuf[rows, :].astype(jnp.float32)
            scale = lax.rsqrt(jnp.mean(wide * wide, axis=1, keepdims=True) + EPS)
            xbuf[rows, :] = (wide * scale * gain[...]).astype(jnp.bfloat16)
            return carry

        lax.fori_loop(0, tok_rows // 32, body, 0)

        def hot(i, carry):
            rows = lax.broadcasted_iota(jnp.int32, (BLOCK, tok_rows), 0) + i * BLOCK
            onehot[pl.ds(pl.multiple_of(i * BLOCK, BLOCK), BLOCK), :] = jnp.where(
                rows == dest[...], 1.0, 0.0
            ).astype(jnp.bfloat16)
            return carry

        lax.fori_loop(0, REGIONS, hot, 0)

    def project(j):
        def body(t, carry):
            at = pl.multiple_of(t * TILE, TILE)
            weights = wbuf[j, :, :, :, :, :, pl.ds(at, TILE)].reshape(features, TILE)
            raw = jnp.dot(xbuf[...], weights, preferred_element_type=jnp.float32)
            if j < per_kind:
                heads = []
                for head in range(TILE // HEAD):
                    one = raw[:, head * HEAD : (head + 1) * HEAD]
                    heads.append(
                        one * cosine[...] + pltpu.roll(one, HEAD // 2, 1) * sine[...]
                    )
                raw = jnp.concatenate(heads, axis=1)
            placed = jnp.dot(
                onehot[...], raw.astype(jnp.bfloat16), preferred_element_type=jnp.float32
            )
            pbuf[j, :, pl.ds(at, TILE)] = placed.astype(jnp.bfloat16)
            return carry

        lax.fori_loop(0, width // TILE, body, 0)

    def spot(j, region):
        rows = pl.ds(region * BLOCK, BLOCK)
        return (
            pbuf.at[j, rows, :],
            out.at[j // per_kind, rows, pl.ds((j % per_kind) * width, width)],
        )

    def hand_over(j):
        for region in (0, 4, 1, 3, 2):
            src, dst = spot(j, region)
            if region == REACH:
                pltpu.make_async_copy(src, dst, hr.at[j, region]).start()
            else:
                send(src, hs.at[j, region], hr.at[j, region], group,
                     lax.rem(me + region - REACH + n, n), dst)

    for j in range(chunks):
        along_z(j)
    spread(0)
    normalise()
    spread(1)
    relay(0)
    for j in range(chunks):
        if j + 2 < chunks:
            spread(j + 2)
        if j + 1 < chunks:
            relay(j + 1)
        finish(j)
        project(j)
        hand_over(j)

    for j in range(chunks):
        wait(wbuf.at[j, 1:, y, core, group], zs.at[j])
        wait(wbuf.at[j, :, y, core, group], ys.at[j])
        wait(wbuf.at[j, 1:, y, core, group], xs.at[j])
        wait(wbuf.at[j, :, other_y, core, group], ds.at[j])
        wait(wbuf.at[j, :, :, core], cs.at[j])
        for region in range(REGIONS):
            src, dst = spot(j, region)
            wait(dst, hr.at[j, region])
            if region != REACH:
                wait(src, hs.at[j, region])


def on_device(n, tokens, norm_gain, w_key, w_value, lengths, page_table):
    device_index = lax.axis_index("seq")
    tok_rows, features = tokens.shape
    columns = w_key.shape[1]
    length_each = tok_rows * n // 2
    token_index = device_index * tok_rows + jnp.arange(tok_rows, dtype=jnp.int32)
    position = token_index % length_each
    limit = jnp.where(token_index // length_each == 0, lengths[0], lengths[1])
    row = (page_table % SLOTS)[:, None] * PAGE + jnp.arange(PAGE, dtype=jnp.int32)[None, :]
    dest = jnp.where(position < limit, row.reshape(tok_rows), -1)[None, :]
    half_head = HEAD // 2
    freq = ROPE_THETA ** (-(jnp.arange(half_head, dtype=jnp.float32) * 2.0 / HEAD))
    angle = position.astype(jnp.float32)[:, None] * freq[None, :]
    angle = jnp.concatenate([angle, angle], axis=1)
    sign = jnp.where(jnp.arange(HEAD) < half_head, -1.0, 1.0).astype(jnp.float32)
    cosine = jnp.cos(angle)
    sine = jnp.sin(angle) * sign[None, :]
    gain = norm_gain.astype(jnp.float32)[None, :]
    depth = n // 4
    half = w_key.shape[0] // 2
    width = 2 * columns // CHUNKS
    dma = pltpu.SemaphoreType.DMA
    vmem = pl.BlockSpec(memory_space=pltpu.VMEM)
    hbm = pl.BlockSpec(memory_space=pl.ANY)
    cache = pl.pallas_call(
        functools.partial(kernel, n),
        out_shape=jax.ShapeDtypeStruct((2, ROWS, columns), jnp.bfloat16),
        in_specs=[hbm, vmem, hbm, hbm, vmem, vmem, vmem],
        out_specs=hbm,
        scratch_shapes=[
            pltpu.VMEM((CHUNKS, depth, 2, 2, 2, half, width), jnp.bfloat16),
            pltpu.VMEM((tok_rows, features), jnp.bfloat16),
            pltpu.VMEM((CHUNKS, ROWS, width), jnp.bfloat16),
            pltpu.VMEM((ROWS, tok_rows), jnp.bfloat16),
            dma((CHUNKS, 2)),
            dma,
            dma((CHUNKS,)), dma((CHUNKS, depth)),
            dma((CHUNKS,)), dma((CHUNKS, depth)),
            dma((CHUNKS,)), dma((CHUNKS, depth)),
            dma((CHUNKS,)), dma((CHUNKS, depth)),
            dma((CHUNKS,)), dma((CHUNKS,)),
            dma((CHUNKS, REGIONS)), dma((CHUNKS, REGIONS)),
        ],
        compiler_params=pltpu.CompilerParams(
            collective_id=0, has_side_effects=True, vmem_limit_bytes=60 * 2**20
        ),
    )(tokens, gain, w_key, w_value, dest, cosine, sine)
    return cache.reshape(2, SLOTS, PAGE, columns)


def solution(mesh):
    placed = (
        P(("group", "seq"), None),
        P(),
        P("seq", None),
        P("seq", None),
        P("group"),
        P(("group", "seq")),
    )
    return jax.shard_map(
        functools.partial(on_device, mesh.shape["seq"]),
        mesh=mesh,
        in_specs=placed,
        out_specs=P(None, ("group", "seq"), None, None),
        check_vma=False,
    )
```

time: 226 us -> 135 us (0.60)
  the two profiles are of different devices: /device:TPU:1 before, /device:TPU:9 now
where the time goes in v1:
time: 135 us
  Pallas kernels  124 us (92%)
  other arithmetic  5.91 us (4%)
  local copies, waits for them, and re-layouts  5.09 us (4%)
    pallas_call x1, Pallas kernels, on_device(): pl.pallas_call(functools.partial(kernel, n), out_shape=jax.ShapeDtypeStru...  124 us
    unnamed x1, local copies, waits for them, and re-layouts  3.67 us

profile of v1, /device:TPU:9, one launch (start us, length us, event | category | flops | bytes accessed | tf_op | source)
XLA Modules:
  0.0 134.5 jit_solution(4257080804886548639)
XLA Ops:
  0.0 0.7 fusion.3
  0.7 1.3 fusion.4
  2.0 0.1 iota_add_fusion
  2.1 0.1 add.85
  2.2 1.9 %compare_select_fusion.dest = s32[1,512]{1,0:T(1,128)} fusion(s32[1,512]{1,0:T(1,128)S(1)} %add.85, s32[]{:T(128)} %bitcast.2, s32[]{:T(128)} %bitcast.1, s32[]{:T(128)S(6)} %mul.34), kind=kLoop, calls=%fused_computation.5 | loop fusion | flops 12288 | bytes 4108 | tf_op jit(solution)/shard_map/jit(_where)/select_n | solution.py:253
  4.1 1.3 broadcast_in_dim.35
  5.4 0.1 broadcast_multiply_fusion
  5.5 1.8 %sine_multiply_fusion = (f32[512,128]{1,0:T(8,128)}, f32[512,128]{1,0:T(8,128)}) fusion(f32[512,64]{1,0:T(8,128)S(1)} %broadcast_multiply_fusion, f32[128]{0:T(128)S(1)} %compare_select_fusion.5), kind=kLoop, calls=%fused_computation.1 | loop fusion | flops 131072 | bytes 655872 | tf_op jit(solution)/shard_map/mul | solution.py:260
  7.3 123.5 %shard_map.64 = bf16[2,640,1024]{2,1,0:T(8,128)(2,1)} custom-call(bf16[512,4096]{1,0:T(8,128)(2,1)} %tokens.1, f32[1,4096]{1,0:T(1,128)} %bitcast.5, bf16[256,1024]{1,0:T(8,128)(2,1)} %w_key.1, bf16[256,1024]{1,0:T(8,128)(2,1)} %w_value.1, s32[1,512]{1,0:T(1,128)} %compare_select_fusion.dest, f32[512,128]{1,0:T(8,128)} %get-tuple-element.6.cosine, ...), custom_call_target="tpu_custom_call" | custom-call | tf_op jit(solution)/shard_map/pallas_call | solution.py:268
  130.9 3.7 %copy.8 = bf16[2,40,16,1024]{3,2,1,0:T(8,128)(2,1)} copy(bf16[2,40,16,1024]{3,2,1,0:T(8,128)(2,1)} %bitcast.4) | data formatting | bytes 5242880
  (3 shorter events, 0.0 us)

commit v2 on v1

v2 whole, which is shorter than its diff:
```python
import functools

import jax
import jax.numpy as jnp
from jax import lax
from jax.experimental import pallas as pl
from jax.experimental.pallas import tpu as pltpu
from jax.sharding import PartitionSpec as P

HEAD = 128
PAGE = 16
REACH = 2
CAP = 8
SLOTS = 40
REGIONS = 2 * REACH + 1
BLOCK = CAP * PAGE
ROWS = SLOTS * PAGE

ROPE_THETA = 500000.0
EPS = 1e-05

CHUNKS = 8
TILE = 256
WAVE = 8
MESH = pl.DeviceIdType.MESH


def kernel(
    n, tokens, gain, w_key, w_value, lengths, pages, freq, out,
    wbuf, xbuf, pbuf, onehot, cosine, sine,
    load_sem, tok_sem, ys, yr, zs, zr, xs, xr, cs, cr, hs, hr,
):
    chunks, depth = wbuf.shape[0], wbuf.shape[1]
    half, width = wbuf.shape[5], wbuf.shape[6]
    per_kind = chunks // 2
    tok_rows, features = xbuf.shape
    group = lax.axis_index("group")
    me = lax.axis_index("seq")
    core, y, z = lax.rem(me, 2), lax.rem(me // 2, 2), me // 4
    other_core, other_y, other_group = 1 - core, 1 - y, 1 - group

    def seq_of(z_at, y_at, core_at):
        return (z_at * 2 + y_at) * 2 + core_at

    def piece(j, z_at, y_at, part):
        return wbuf.at[j, z_at, y_at, core, part]

    def send(ref, send_sem, recv_sem, group_at, seq_at, dst=None):
        pltpu.make_async_remote_copy(
            src_ref=ref,
            dst_ref=ref if dst is None else dst,
            send_sem=send_sem,
            recv_sem=recv_sem,
            device_id={"group": group_at, "seq": seq_at},
            device_id_type=MESH,
        ).start()

    def wait(ref, sem):
        pltpu.make_async_copy(ref, ref, sem).wait()

    loads = []
    for j in range(chunks):
        w_ref = w_key if j < per_kind else w_value
        columns = pl.ds((j % per_kind) * width, width)
        for part in range(2):
            copy = pltpu.make_async_copy(
                w_ref.at[pl.ds(part * half, half), columns],
                wbuf.at[j, z, y, core, part],
                load_sem.at[j, part],
            )
            copy.start()
            loads.append(copy)
    token_copy = pltpu.make_async_copy(tokens, xbuf, tok_sem)
    token_copy.start()

    to_y = seq_of(z, other_y, core)
    to_core = seq_of(z, y, other_core)
    has_up, has_down = z + 1 < depth, z > 0
    up = seq_of(lax.rem(z + 1, depth), y, core)
    down = seq_of(lax.rem(z + depth - 1, depth), y, core)

    barrier = pltpu.get_barrier_semaphore()

    def greet(group_at, seq_at):
        pl.semaphore_signal(
            barrier, inc=1, device_id={"group": group_at, "seq": seq_at}, device_id_type=MESH
        )

    greet(group, up)
    greet(group, down)
    greet(group, to_y)
    greet(group, to_core)
    greet(other_group, me)
    for region in range(REGIONS):
        if region != REACH:
            greet(group, lax.rem(me + region - REACH + n, n))
    pl.semaphore_wait(barrier, 5 + REGIONS - 1)

    def to_partner(j, ref):
        send(ref, cs.at[j], cr.at[j], group, to_core)

    def go_up(j, z_at, y_at, k):
        @pl.when(has_up)
        def _():
            send(piece(j, z_at, y_at, group), zs.at[j, 0, k], zr.at[j, y_at, z_at], group, up)

    def go_down(j, z_at, y_at, k):
        @pl.when(has_down)
        def _():
            send(piece(j, z_at, y_at, group), zs.at[j, 1, k], zr.at[j, y_at, z_at], group, down)

    def begin(j):
        for part in (0, 1):
            ref = piece(j, z, y, part)
            send(ref, ys.at[j], yr.at[j, part], group, to_y)
        go_up(j, z, y, 0)
        go_down(j, z, y, 0)
        for part in (0, 1):
            to_partner(j, piece(j, z, y, part))

    def cross(j):
        for part in (0, 1):
            wait(piece(j, z, other_y, part), yr.at[j, part])
        go_up(j, z, other_y, 0)
        go_down(j, z, other_y, 0)
        for part in (0, 1):
            to_partner(j, piece(j, z, other_y, part))

    def arrive(j, z_at, y_at):
        ref = piece(j, z_at, y_at, group)
        wait(ref, zr.at[j, y_at, z_at])
        return ref

    def pass_on(j, ref, z_at, y_at):
        send(ref, xs.at[j], xr.at[j, y_at, z_at], other_group, me)
        to_partner(j, ref)

    def along(j, k):
        for y_at in (y, other_y):
            @pl.when(z - k >= 0)
            def _():
                ref = arrive(j, z - k, y_at)
                go_up(j, z - k, y_at, k)
                pass_on(j, ref, z - k, y_at)

            @pl.when(z + k < depth)
            def _():
                ref = arrive(j, z + k, y_at)
                go_down(j, z + k, y_at, k)
                pass_on(j, ref, z + k, y_at)

    def finish(j):
        def body(k, carry):
            for y_at in (y, other_y):
                @pl.when(z - k >= 0)
                def _():
                    ref = piece(j, z - k, y_at, other_group)
                    wait(ref, xr.at[j, y_at, z - k])
                    to_partner(j, ref)

                @pl.when(z + k < depth)
                def _():
                    ref = piece(j, z + k, y_at, other_group)
                    wait(ref, xr.at[j, y_at, z + k])
                    to_partner(j, ref)

            return carry

        lax.fori_loop(1, depth, body, 0)

    def prepare():
        token_copy.wait()
        length_each = tok_rows * n // 2

        def body(i, carry):
            rows = pl.ds(pl.multiple_of(i * 32, 32), 32)
            wide = xbuf[rows, :].astype(jnp.float32)
            scale = lax.rsqrt(jnp.mean(wide * wide, axis=1, keepdims=True) + EPS)
            xbuf[rows, :] = (wide * scale * gain[...].astype(jnp.float32)).astype(jnp.bfloat16)
            return carry

        lax.fori_loop(0, tok_rows // 32, body, 0)

        first = lax.rem(me * tok_rows, length_each)
        second_prompt = (me * tok_rows) // length_each
        limit = lengths[0] + second_prompt * (lengths[1] - lengths[0])
        page_count = tok_rows // PAGE
        token = lax.broadcasted_iota(jnp.int32, (page_count, tok_rows), 1)
        page = lax.broadcasted_iota(jnp.int32, (page_count, tok_rows), 0)
        used = jnp.where((token // PAGE == page) & (first + token < limit), 1.0, 0.0)
        used = used.astype(jnp.bfloat16)
        slot = lax.rem(pages[...], SLOTS)

        def hot(i, carry):
            at = i * BLOCK
            row = lax.broadcasted_iota(jnp.int32, (BLOCK, page_count), 0) + at
            held = jnp.where(row // PAGE == slot, 1.0, 0.0).astype(jnp.bfloat16)
            spread = jnp.dot(held, used, preferred_element_type=jnp.float32)
            row = lax.broadcasted_iota(jnp.int32, (BLOCK, tok_rows), 0)
            column = lax.broadcasted_iota(jnp.int32, (BLOCK, tok_rows), 1)
            same = lax.rem(row, PAGE) == lax.rem(column, PAGE)
            onehot[pl.ds(pl.multiple_of(at, BLOCK), BLOCK), :] = jnp.where(
                same, spread, 0.0
            ).astype(jnp.bfloat16)
            return carry

        lax.fori_loop(0, REGIONS, hot, 0)

        def turn(i, carry):
            at = pl.multiple_of(i * 64, 64)
            row = lax.broadcasted_iota(jnp.int32, (64, HEAD), 0) + (first + at)
            lane = lax.broadcasted_iota(jnp.int32, (64, HEAD), 1)
            angle = row.astype(jnp.float32) * freq[...]
            cosine[pl.ds(at, 64), :] = jnp.cos(angle)
            sined = jnp.sin(angle)
            sine[pl.ds(at, 64), :] = jnp.where(lane < HEAD // 2, -sined, sined)
            return carry

        lax.fori_loop(0, tok_rows // 64, turn, 0)

    def project(j):
        wait(wbuf.at[j, :, :, other_core], cr.at[j])
        for t in range(width // TILE):
            at = t * TILE
            weights = wbuf[j, :, :, :, :, :, at : at + TILE].reshape(features, TILE)
            raw = jnp.dot(xbuf[...], weights, preferred_element_type=jnp.float32)
            if j < per_kind:
                heads = []
                for head in range(TILE // HEAD):
                    one = raw[:, head * HEAD : (head + 1) * HEAD]
                    heads.append(
                        one * cosine[...] + pltpu.roll(one, HEAD // 2, 1) * sine[...]
                    )
                raw = jnp.concatenate(heads, axis=1)
            placed = jnp.dot(
                onehot[...], raw.astype(jnp.bfloat16), preferred_element_type=jnp.float32
            )
            pbuf[j, :, at : at + TILE] = placed.astype(jnp.bfloat16)

    def spot(j, region):
        rows = pl.ds(region * BLOCK, BLOCK)
        return (
            pbuf.at[j, rows, :],
            out.at[j // per_kind, rows, pl.ds((j % per_kind) * width, width)],
        )

    def hand_over(j):
        for region in (0, 4, 1, 3, 2):
            src, dst = spot(j, region)
            if region == REACH:
                pltpu.make_async_copy(src, dst, hr.at[j, region]).start()
            else:
                send(src, hs.at[j, region], hr.at[j, region], group,
                     lax.rem(me + region - REACH + n, n), dst)

    def stage(j, k):
        if k == 0:
            cross(j)
        else:
            along(j, k)

    for j in range(chunks):
        for copy in loads[2 * j : 2 * j + 2]:
            copy.wait()
        begin(j)
    if depth <= WAVE:
        for t in range(chunks + depth + 1):
            for j in range(chunks):
                k = t - j
                if 0 <= k < depth:
                    stage(j, k)
            if t == 1:
                prepare()
            if 0 <= t - depth < chunks:
                finish(t - depth)
            if 0 <= t - depth - 1 < chunks:
                project(t - depth - 1)
                hand_over(t - depth - 1)
    else:
        prepare()
        for j in range(chunks):
            stage(j, 0)
            lax.fori_loop(1, depth, lambda k, carry: (along(j, k), carry)[1], 0)
            finish(j)
            project(j)
            hand_over(j)

    for j in range(chunks):
        wait(wbuf.at[j, z, y, core], ys.at[j])
        wait(wbuf.at[j, 1:, :, core, group], xs.at[j])
        wait(wbuf.at[j, :, :, core], cs.at[j])

        def drain(k, carry):
            @pl.when(has_up & (z - k >= 0))
            def _():
                wait(wbuf.at[j, 0, :, core, group], zs.at[j, 0, k])

            @pl.when(has_down & (z + k < depth))
            def _():
                wait(wbuf.at[j, 0, :, core, group], zs.at[j, 1, k])

            return carry

        lax.fori_loop(0, depth, drain, 0)
        for region in range(REGIONS):
            src, dst = spot(j, region)
            wait(dst, hr.at[j, region])
            if region != REACH:
                wait(src, hs.at[j, region])


def on_device(n, tokens, norm_gain, w_key, w_value, lengths, page_table):
    tok_rows, features = tokens.shape
    columns = w_key.shape[1]
    freq = ROPE_THETA ** (-(jnp.arange(HEAD // 2, dtype=jnp.float32) * 2.0 / HEAD))
    freq = jnp.concatenate([freq, freq])[None, :]
    depth = n // 4
    half = w_key.shape[0] // 2
    width = 2 * columns // CHUNKS
    dma = pltpu.SemaphoreType.DMA
    vmem = pl.BlockSpec(memory_space=pltpu.VMEM)
    smem = pl.BlockSpec(memory_space=pltpu.SMEM)
    hbm = pl.BlockSpec(memory_space=pl.ANY)
    cache = pl.pallas_call(
        functools.partial(kernel, n),
        out_shape=jax.ShapeDtypeStruct((2, ROWS, columns), jnp.bfloat16),
        in_specs=[hbm, vmem, hbm, hbm, smem, vmem, vmem],
        out_specs=hbm,
        scratch_shapes=[
            pltpu.VMEM((CHUNKS, depth, 2, 2, 2, half, width), jnp.bfloat16),
            pltpu.VMEM((tok_rows, features), jnp.bfloat16),
            pltpu.VMEM((CHUNKS, ROWS, width), jnp.bfloat16),
            pltpu.VMEM((ROWS, tok_rows), jnp.bfloat16),
            pltpu.VMEM((tok_rows, HEAD), jnp.float32),
            pltpu.VMEM((tok_rows, HEAD), jnp.float32),
            dma((CHUNKS, 2)),
            dma,
            dma((CHUNKS,)), dma((CHUNKS, 2)),
            dma((CHUNKS, 2, depth)), dma((CHUNKS, 2, depth)),
            dma((CHUNKS,)), dma((CHUNKS, 2, depth)),
            dma((CHUNKS,)), dma((CHUNKS,)),
            dma((CHUNKS, REGIONS)), dma((CHUNKS, REGIONS)),
        ],
        compiler_params=pltpu.CompilerParams(
            collective_id=0, has_side_effects=True, vmem_limit_bytes=60 * 2**20
        ),
    )(tokens, norm_gain[None, :], w_key, w_value, lengths, page_table[None, :], freq)
    return cache.reshape(2, SLOTS, PAGE, columns)


def solution(mesh):
    placed = (
        P(("group", "seq"), None),
        P(),
        P("seq", None),
        P("seq", None),
        P("group"),
        P(("group", "seq")),
    )
    return jax.shard_map(
        functools.partial(on_device, mesh.shape["seq"]),
        mesh=mesh,
        in_specs=placed,
        out_specs=P(None, ("group", "seq"), None, None),
        check_vma=False,
    )
```

time: 135 us -> 112 us (0.83)
  the two profiles are of different devices: /device:TPU:9 before, /device:TPU:1 now
where the time goes in v2:
time: 112 us
  Pallas kernels  106 us (95%)
  local copies, waits for them, and re-layouts  4.98 us (4%)
    pallas_call x1, Pallas kernels, on_device(): pl.pallas_call(functools.partial(kernel, n), out_shape=jax.ShapeDtypeStru...  106 us
    unnamed x1, local copies, waits for them, and re-layouts  3.67 us

profile of v2, /device:TPU:1, one launch (start us, length us, event | category | flops | bytes accessed | tf_op | source)
XLA Modules:
  0.0 111.6 jit_solution(15518693993659193974)
XLA Ops:
  0.0 0.6 maximum_bitcast_fusion.freq
  0.6 1.3 %broadcast_in_dim.9.gain = bf16[1,4096]{1,0:T(2,128)(2,1)} reshape(bf16[4096]{0:T(1024)(128)(2,1)} %param.7) | data formatting | bytes 16384 | tf_op jit(solution)/shard_map/broadcast_in_dim | solution.py:347
  1.9 106.0 %shard_map.64 = bf16[2,640,1024]{2,1,0:T(8,128)(2,1)} custom-call(bf16[512,4096]{1,0:T(8,128)(2,1)} %tokens.1, bf16[1,4096]{1,0:T(2,128)(2,1)} %broadcast_in_dim.9.gain, bf16[256,1024]{1,0:T(8,128)(2,1)} %w_key.1, bf16[256,1024]{1,0:T(8,128)(2,1)} %w_value.1, s32[2]{0:T(128)} %lengths.1, s32[1,32]{1,0:T(1,128)} %bitcast.5, f32[1,128]{1,0:T(1,128)} %maximum_bitcast_fusion.freq), custom_call_target="tpu_custom_call" | custom-call | tf_op jit(solution)/shard_map/pallas_call | solution.py:324
  107.9 3.7 %copy.8 = bf16[2,40,16,1024]{3,2,1,0:T(8,128)(2,1)} copy(bf16[2,40,16,1024]{3,2,1,0:T(8,128)(2,1)} %bitcast.4) | data formatting | bytes 5242880
  (1 shorter events, 0.0 us)

commit v3 on v2

--- a/solution.py
+++ b/solution.py
@@ -2,6 +2,7 @@
 
 import jax
 import jax.numpy as jnp
+import numpy as np
 from jax import lax
 from jax.experimental import pallas as pl
 from jax.experimental.pallas import tpu as pltpu
@@ -22,13 +23,15 @@
 CHUNKS = 8
 TILE = 256
 WAVE = 8
+LAG = 2
+MIXED = (0, 2, 4)
 MESH = pl.DeviceIdType.MESH
 
 
 def kernel(
     n, tokens, gain, w_key, w_value, lengths, pages, freq, out,
     wbuf, xbuf, pbuf, onehot, cosine, sine,
-    load_sem, tok_sem, ys, yr, zs, zr, xs, xr, cs, cr, hs, hr,
+    load_sem, tok_sem, ys, yr, fr, zs, zr, xs, xr, cs, cr, hs, hr,
 ):
     chunks, depth = wbuf.shape[0], wbuf.shape[1]
     half, width = wbuf.shape[5], wbuf.shape[6]
@@ -121,8 +124,9 @@
     def cross(j):
         for part in (0, 1):
             wait(piece(j, z, other_y, part), yr.at[j, part])
-        go_up(j, z, other_y, 0)
-        go_down(j, z, other_y, 0)
+        if j not in MIXED:
+            go_up(j, z, other_y, 0)
+            go_down(j, z, other_y, 0)
         for part in (0, 1):
             to_partner(j, piece(j, z, other_y, part))
 
@@ -134,9 +138,14 @@
     def pass_on(j, ref, z_at, y_at):
         send(ref, xs.at[j], xr.at[j, y_at, z_at], other_group, me)
         to_partner(j, ref)
+        if j in MIXED:
+            send(ref, ys.at[j], fr.at[j, 0, z_at], group, to_y)
+
+    def lines(j):
+        return (y,) if j in MIXED else (y, other_y)
 
     def along(j, k):
-        for y_at in (y, other_y):
+        for y_at in lines(j):
             @pl.when(z - k >= 0)
             def _():
                 ref = arrive(j, z - k, y_at)
@@ -149,39 +158,58 @@
                 go_down(j, z + k, y_at, k)
                 pass_on(j, ref, z + k, y_at)
 
+    def others(visit):
+        def body(k, carry):
+            @pl.when(z - k >= 0)
+            def _():
+                visit(z - k)
+
+            @pl.when(z + k < depth)
+            def _():
+                visit(z + k)
+
+            return carry
+
+        lax.fori_loop(1, depth, body, 0)
+
     def finish(j):
-        def body(k, carry):
-            for y_at in (y, other_y):
-                @pl.when(z - k >= 0)
-                def _():
-                    ref = piece(j, z - k, y_at, other_group)
-                    wait(ref, xr.at[j, y_at, z - k])
-                    to_partner(j, ref)
-
-                @pl.when(z + k < depth)
-                def _():
-                    ref = piece(j, z + k, y_at, other_group)
-                    wait(ref, xr.at[j, y_at, z + k])
-                    to_partner(j, ref)
-
-            return carry
-
-        lax.fori_loop(1, depth, body, 0)
-
-    def prepare():
-        token_copy.wait()
-        length_each = tok_rows * n // 2
-
+        def visit(zz):
+            for y_at in lines(j):
+                ref = piece(j, zz, y_at, other_group)
+                wait(ref, xr.at[j, y_at, zz])
+                if j in MIXED:
+                    send(ref, ys.at[j], fr.at[j, 1, zz], group, to_y)
+                to_partner(j, ref)
+            if j in MIXED:
+                ref = piece(j, zz, other_y, group)
+                wait(ref, fr.at[j, 0, zz])
+                to_partner(j, ref)
+
+        others(visit)
+
+    def settle(j):
+        def visit(zz):
+            ref = piece(j, zz, other_y, other_group)
+            wait(ref, fr.at[j, 1, zz])
+            to_partner(j, ref)
+
+        if j in MIXED:
+            others(visit)
+
+    length_each = tok_rows * n // 2
+    first = lax.rem(me * tok_rows, length_each)
+
+    def normalise(at, rows_here):
         def body(i, carry):
-            rows = pl.ds(pl.multiple_of(i * 32, 32), 32)
+            rows = pl.ds(pl.multiple_of(at + i * 32, 32), 32)
             wide = xbuf[rows, :].astype(jnp.float32)
             scale = lax.rsqrt(jnp.mean(wide * wide, axis=1, keepdims=True) + EPS)
             xbuf[rows, :] = (wide * scale * gain[...].astype(jnp.float32)).astype(jnp.bfloat16)
             return carry
 
-        lax.fori_loop(0, tok_rows // 32, body, 0)
-
-        first = lax.rem(me * tok_rows, length_each)
+        lax.fori_loop(0, rows_here // 32, body, 0)
+
+    def mark_rows():
         second_prompt = (me * tok_rows) // length_each
         limit = lengths[0] + second_prompt * (lengths[1] - lengths[0])
         page_count = tok_rows // PAGE
@@ -206,6 +234,7 @@
 
         lax.fori_loop(0, REGIONS, hot, 0)
 
+    def angles():
         def turn(i, carry):
             at = pl.multiple_of(i * 64, 64)
             row = lax.broadcasted_iota(jnp.int32, (64, HEAD), 0) + (first + at)
@@ -263,41 +292,56 @@
         for copy in loads[2 * j : 2 * j + 2]:
             copy.wait()
         begin(j)
+    quarter = tok_rows // 4
+    jobs = [token_copy.wait]
+    jobs += [functools.partial(normalise, i * quarter, quarter) for i in range(4)]
+    jobs += [mark_rows, angles]
     if depth <= WAVE:
-        for t in range(chunks + depth + 1):
+        for t in range(chunks + depth + LAG):
             for j in range(chunks):
                 k = t - j
                 if 0 <= k < depth:
                     stage(j, k)
-            if t == 1:
-                prepare()
+            for job in jobs[2 * t : 2 * t + 2]:
+                job()
             if 0 <= t - depth < chunks:
                 finish(t - depth)
             if 0 <= t - depth - 1 < chunks:
-                project(t - depth - 1)
-                hand_over(t - depth - 1)
+                settle(t - depth - 1)
+            if 0 <= t - depth - LAG < chunks:
+                project(t - depth - LAG)
+                hand_over(t - depth - LAG)
     else:
-        prepare()
+        for job in jobs:
+            job()
         for j in range(chunks):
             stage(j, 0)
             lax.fori_loop(1, depth, lambda k, carry: (along(j, k), carry)[1], 0)
             finish(j)
+            settle(j)
             project(j)
             hand_over(j)
 
     for j in range(chunks):
-        wait(wbuf.at[j, z, y, core], ys.at[j])
-        wait(wbuf.at[j, 1:, :, core, group], xs.at[j])
+        if j in MIXED:
+            wait(wbuf.at[j, :, y, core], ys.at[j])
+            wait(wbuf.at[j, 1:, y, core, group], xs.at[j])
+        else:
+            wait(wbuf.at[j, z, y, core], ys.at[j])
+            wait(wbuf.at[j, 1:, :, core, group], xs.at[j])
+        sent = wbuf.at[j, 0, :, core, group]
+        if j in MIXED:
+            sent = wbuf.at[j, 0, y, core, group]
         wait(wbuf.at[j, :, :, core], cs.at[j])
 
         def drain(k, carry):
             @pl.when(has_up & (z - k >= 0))
             def _():
-                wait(wbuf.at[j, 0, :, core, group], zs.at[j, 0, k])
+                wait(sent, zs.at[j, 0, k])
 
             @pl.when(has_down & (z + k < depth))
             def _():
-                wait(wbuf.at[j, 0, :, core, group], zs.at[j, 1, k])
+                wait(sent, zs.at[j, 1, k])
 
             return carry
 
@@ -312,8 +356,8 @@
 def on_device(n, tokens, norm_gain, w_key, w_value, lengths, page_table):
     tok_rows, features = tokens.shape
     columns = w_key.shape[1]
-    freq = ROPE_THETA ** (-(jnp.arange(HEAD // 2, dtype=jnp.float32) * 2.0 / HEAD))
-    freq = jnp.concatenate([freq, freq])[None, :]
+    freq = ROPE_THETA ** (-(np.arange(HEAD // 2) * 2.0 / HEAD))
+    freq = np.concatenate([freq, freq]).astype(np.float32)[None, :]
     depth = n // 4
     half = w_key.shape[0] // 2
     width = 2 * columns // CHUNKS
@@ -335,7 +379,7 @@
             pltpu.VMEM((tok_rows, HEAD), jnp.float32),
             dma((CHUNKS, 2)),
             dma,
-            dma((CHUNKS,)), dma((CHUNKS, 2)),
+            dma((CHUNKS,)), dma((CHUNKS, 2)), dma((CHUNKS, 2, depth)),
             dma((CHUNKS, 2, depth)), dma((CHUNKS, 2, depth)),
             dma((CHUNKS,)), dma((CHUNKS, 2, depth)),
             dma((CHUNKS,)), dma((CHUNKS,)),

time: 112 us -> 101 us (0.902)
  Pallas kernels: 106 us -> 96.1 us
    pallas_call x1, Pallas kernels: 106 us -> 96.1 us  [on_device(): pl.pallas_call(functools.partial(kernel, n), out_shape=jax.ShapeDtypeStru...]
where the time goes in v3:
time: 101 us
  Pallas kernels  96.1 us (95%)
  local copies, waits for them, and re-layouts  4.98 us (5%)
    pallas_call x1, Pallas kernels, on_device(): pl.pallas_call(functools.partial(kernel, n), out_shape=jax.ShapeDtypeStru...  96.1 us
    unnamed x1, local copies, waits for them, and re-layouts  3.67 us

profile of v3, /device:TPU:1, one launch (start us, length us, event | category | flops | bytes accessed | tf_op | source)
XLA Modules:
  0.0 101.1 jit_solution(2001759398667523018)
XLA Ops:
  0.0 1.3 %broadcast_in_dim.6.gain = bf16[1,4096]{1,0:T(2,128)(2,1)} reshape(bf16[4096]{0:T(1024)(128)(2,1)} %param.8) | data formatting | bytes 16384 | tf_op jit(solution)/shard_map/broadcast_in_dim | solution.py:391
  1.3 96.1 %shard_map.73 = bf16[2,640,1024]{2,1,0:T(8,128)(2,1)} custom-call(bf16[512,4096]{1,0:T(8,128)(2,1)} %tokens.1, bf16[1,4096]{1,0:T(2,128)(2,1)} %broadcast_in_dim.6.gain, bf16[256,1024]{1,0:T(8,128)(2,1)} %w_key.1, bf16[256,1024]{1,0:T(8,128)(2,1)} %w_value.1, s32[2]{0:T(128)} %lengths.1, s32[1,32]{1,0:T(1,128)} %bitcast.3, f32[1,128]{1,0:T(1,128)} %constant.2.clone.freq), custom_call_target="tpu_custom_call" | custom-call | tf_op jit(solution)/shard_map/pallas_call | solution.py:368
  97.5 3.7 %copy.9 = bf16[2,40,16,1024]{3,2,1,0:T(8,128)(2,1)} copy(bf16[2,40,16,1024]{3,2,1,0:T(8,128)(2,1)} %bitcast.2) | data formatting | bytes 5242880
